TPU v7x, 32 devices: a whole 2x2x4 slice. The times are simulated.
32 devices in a mesh: scen: 8 (over y, x, core), col: 4 (over z).
Axes of the slice: x: 2, y: 2, z: 4, core: 2. Of those that a mesh axis runs over, the one named last changes fastest.
Arguments:
- tech: bfloat16 [32, 2048, 4096], P('scen', None, 'col'), may hold values from -0.046875 to 0.046875
- recourse: bfloat16 [32, 2048, 1024], P('scen', None, 'col'), may hold values from -0.125 to 0.125
- rhs: float32 [32, 32, 2048], P(None, 'scen'), may hold values from -6 to 6
- cost_first: float32 [4096], P('col'), may hold values from -6 to 6
- cost_second: float32 [32, 1024], P('scen', 'col'), may hold values from -6 to 6
- cone_id: int32 [32, 2048], P('scen'), may hold values from 0 to 127, never falling along the last dimension, each value on 1 to 64 neighbouring positions
Outputs:
- first_section: float32 [32, 4096], P(None, 'col')
- second_section: float32 [32, 32, 1024], P(None, 'scen', 'col')
- slack: float32 [32, 32, 2048], P(None, 'scen', 'col')
- dual: float32 [32, 32, 2048], P(None, 'scen', 'col')
Inputs may be any that keep to these rules, and one draw needn't show every extreme that they name: Along the rows of a scenario cone_id never falls; a cone holds 1 to 64 rows.
All inputs are finite; a program needn't handle non-finite values.
Results may differ from a plain program's by a relative error of at most 0.014.
Values may be sent and summed in bfloat16 or wider, within the bound.
A program may use at most 128 MiB of HBM per device.

v0:
```python
import jax
import jax.numpy as jnp
from jax import lax
from jax.sharding import PartitionSpec as P

NCONE = 128
ITERS = 3
CG_STEPS = 3


HIGH = lax.Precision.HIGHEST


def cone_factors(lead, tail):
    norm_tail = jnp.sqrt(tail)
    inside = norm_tail <= lead
    polar = norm_tail <= -lead
    safe = jnp.where(norm_tail > 0.0, norm_tail, 1.0)
    middle = 0.5 * (lead + norm_tail)
    head = jnp.where(inside, lead, jnp.where(polar, 0.0, middle))
    scale = jnp.where(inside, 1.0, jnp.where(polar, 0.0, middle / safe))
    return (head, scale)


def body(tech, recourse, rhs, cost_first, cost_second, cone_id):
    f32 = jnp.float32
    bf16 = jnp.bfloat16
    n_scen = lax.axis_size("scen")
    n_col = lax.axis_size("col")
    batch = rhs.shape[0]
    scen_local = tech.shape[0]
    rows = tech.shape[1]
    first_cols = tech.shape[2]
    tech_flat = tech.reshape(scen_local * rows, first_cols)
    starts = jnp.concatenate(
        [jnp.ones((scen_local, 1), f32), (cone_id[:, 1:] != cone_id[:, :-1]).astype(f32)], axis=1
    )
    labels = lax.broadcasted_iota(jnp.int32, (1, 1, NCONE), 2)
    onehot = (cone_id[:, :, None] == labels).astype(f32)
    part_rows = rows // n_col
    row_start = lax.axis_index("col") * part_rows
    row_weight = 1.0 / n_col
    share_cols = first_cols // n_scen
    cost_here = lax.dynamic_slice_in_dim(
        cost_first, lax.axis_index("scen") * share_cols, share_cols, 0
    )
    first_weight = 1.0
    start_rows = starts[None]

    def couple(partial_value):
        return lax.psum_scatter(partial_value, "scen", scatter_dimension=1, tiled=True)

    def adjoint(rows_bf):
        first_part = jnp.dot(
            rows_bf.reshape(batch, scen_local * rows), tech_flat, preferred_element_type=f32
        )
        second_part = jnp.einsum("bsm,smk->bsk", rows_bf, recourse, preferred_element_type=f32)
        return (first_part, second_part)

    def local_squares(first_vec, second_vec):
        return first_weight * jnp.sum(first_vec * first_vec, axis=1) + jnp.sum(
            second_vec * second_vec, axis=(1, 2)
        )

    def total_norm(first_vec, second_vec):
        return lax.psum(local_squares(first_vec, second_vec), ("scen", "col"))

    here_rows = rhs.shape[2]
    first_sol = jnp.zeros((batch, share_cols), f32)
    second_sol = jnp.zeros((batch, scen_local, recourse.shape[2]), f32)
    slack = jnp.zeros((batch, scen_local, here_rows), f32)
    dual = jnp.zeros((batch, scen_local, here_rows), f32)
    image = jnp.zeros((batch, scen_local, here_rows), f32)
    for outer in range(ITERS):
        resid_rows = (rhs - slack - dual - image).astype(bf16)
        back_first, back_second = adjoint(resid_rows)
        res_first = couple(back_first) - cost_here[None, :]
        res_second = back_second - cost_second[None]
        res_norm = total_norm(res_first, res_second)
        dir_first, dir_second = (res_first, res_second)
        for step in range(CG_STEPS):
            dir_first_bf = lax.all_gather(dir_first.astype(bf16), "scen", axis=1, tiled=True)
            forward_partial_value = lax.dot_general(
                dir_first_bf, tech_flat, (((1,), (1,)), ((), ())), preferred_element_type=f32
            )
            forward_partial_value = forward_partial_value.reshape(batch, scen_local, rows)
            image_step = lax.psum(
                forward_partial_value
                + jnp.einsum(
                    "bsk,smk->bsm", dir_second.astype(bf16), recourse, preferred_element_type=f32
                ),
                "col",
            )
            curv_term = local_squares(dir_first, dir_second) + row_weight * jnp.sum(
                image_step * image_step, axis=(1, 2)
            )
            curv = lax.psum(curv_term, ("scen", "col"))
            alpha = res_norm / curv
            first_sol = first_sol + alpha[:, None] * dir_first
            second_sol = second_sol + alpha[:, None, None] * dir_second
            image = image + alpha[:, None, None] * image_step
            if step + 1 < CG_STEPS:
                back_first, back_second = adjoint(image_step.astype(bf16))
                res_first = res_first - alpha[:, None] * (dir_first + couple(back_first))
                res_second = res_second - alpha[:, None, None] * (dir_second + back_second)
                new_norm = total_norm(res_first, res_second)
                ratio = new_norm / res_norm
                dir_first = res_first + ratio[:, None] * dir_first
                dir_second = res_second + ratio[:, None, None] * dir_second
                res_norm = new_norm
        values = rhs - image - dual
        project_lead = jnp.einsum("bsm,smc->bsc", values * start_rows, onehot, precision=HIGH)
        project_tail = jnp.einsum(
            "bsm,smc->bsc", values * values * (1.0 - start_rows), onehot, precision=HIGH
        )
        project_lead, project_tail = (project_lead, project_tail)
        head, scale = cone_factors(project_lead, project_tail)
        head_rows = jnp.einsum("bsc,smc->bsm", head, onehot, precision=HIGH)
        scale_rows = jnp.einsum("bsc,smc->bsm", scale, onehot, precision=HIGH)
        slack = start_rows * head_rows + (1.0 - start_rows) * values * scale_rows
        dual = dual + image + slack - rhs
    first_out = lax.all_gather(first_sol, "scen", axis=1, tiled=True)
    slack_out = lax.dynamic_slice_in_dim(slack, row_start, part_rows, 2)
    dual_out = lax.dynamic_slice_in_dim(dual, row_start, part_rows, 2)
    return (first_out, second_sol, slack_out, dual_out)


def solution(mesh):
    placed = (
        P("scen", None, "col"),
        P("scen", None, "col"),
        P(None, "scen", None),
        P("col"),
        P("scen", "col"),
        P("scen", None),
    )
    return jax.shard_map(
        body,
        mesh=mesh,
        in_specs=placed,
        out_specs=(
            P(None, "col"),
            P(None, "scen", "col"),
            P(None, "scen", "col"),
            P(None, "scen", "col"),
        ),
        check_vma=False,
    )
```

profile of v0, /device:TPU:0, one launch (start us, length us, event | category | flops | bytes accessed | tf_op | source)
XLA Modules:
  0.0 1593.4 jit_solution(15257409397023678679)
XLA Ops:
  22.1 32.4 %reduce-scatter.10.cloned.1.call-done = f32[32,128]{1,0:T(8,128)} async-done(((f32[32,1024]{1,0:T(8,128)}), f32[32,128]{1,0:T(8,128)}) %reduce-scatter.10.cloned.1.call-update) | async-done | bytes 16400 | tf_op jit(solution)/shard_map/reduce_scatter | solution.py:51
  64.2 12.0 fusion.136
  79.9 52.0 %all-reduce.14.cloned.1.call-done = f32[32,4,2048]{2,0,1:T(8,128)} async-done(((f32[32,4,2048]{2,0,1:T(8,128)}), f32[32,4,2048]{2,0,1:T(8,128)}) %all-reduce.14.cloned.1.call-update) | async-done | bytes 1048592 | tf_op jit(solution)/shard_map/psum | solution.py:87
  142.0 40.0 %all-reduce.3 = (f32[32]{0:T(128)S(1)}, f32[32]{0:T(128)S(1)}) all-reduce(f32[32]{0:T(128)S(1)} %get-tuple-element.49, f32[32]{0:T(128)S(1)} %get-tuple-element.48), channel_id=1, replica_groups=mesh['scen'=8,'col'=4] {'scen','col'}, use_global_device_ids=true, to_apply=%region_3.0 | all-reduce | flops 64 | bytes 512 | tf_op jit(solution)/shard_map/psum | solution.py:66
  186.0 39.4 %psum.192 = f32[32]{0:T(128)S(1)} all-reduce(f32[32]{0:T(128)S(1)} %add.364), channel_id=1, replica_groups=mesh['scen'=8,'col'=4] {'scen','col'}, use_global_device_ids=true, to_apply=%region_10.0 | all-reduce | flops 32 | bytes 256 | tf_op jit(solution)/shard_map/psum | solution.py:66
  235.3 11.9 fusion.134
  251.0 50.4 %all-reduce.16.cloned.1.call-done = f32[32,4,2048]{2,0,1:T(8,128)} async-done(((f32[32,4,2048]{2,0,1:T(8,128)}), f32[32,4,2048]{2,0,1:T(8,128)}) %all-reduce.16.cloned.1.call-update) | async-done | bytes 1048592 | tf_op jit(solution)/shard_map/psum | solution.py:87
  312.7 40.0 %psum.194 = f32[32]{0:T(128)S(1)} all-reduce(f32[32]{0:T(128)S(1)} %multiply_add_fusion.27), channel_id=1, replica_groups=mesh['scen'=8,'col'=4] {'scen','col'}, use_global_device_ids=true, to_apply=%region_15.0 | all-reduce | flops 32 | bytes 256 | tf_op jit(solution)/shard_map/psum | solution.py:97
  356.8 39.2 %psum.195 = f32[32]{0:T(128)S(1)} all-reduce(f32[32]{0:T(128)S(1)} %add.373), channel_id=1, replica_groups=mesh['scen'=8,'col'=4] {'scen','col'}, use_global_device_ids=true, to_apply=%region_19.0 | all-reduce | flops 32 | bytes 256 | tf_op jit(solution)/shard_map/psum | solution.py:66
  422.9 50.0 %all-reduce.18.cloned.1.call-done = f32[32,4,2048]{2,0,1:T(8,128)} async-done(((f32[32,4,2048]{2,0,1:T(8,128)}), f32[32,4,2048]{2,0,1:T(8,128)}) %all-reduce.18.cloned.1.call-update) | async-done | bytes 1048592 | tf_op jit(solution)/shard_map/psum | solution.py:87
  474.5 40.0 %psum.197 = f32[32]{0:T(128)S(1)} all-reduce(f32[32]{0:T(128)S(1)} %multiply_add_fusion.26), channel_id=1, replica_groups=mesh['scen'=8,'col'=4] {'scen','col'}, use_global_device_ids=true, to_apply=%region_24.0 | all-reduce | flops 32 | bytes 256 | tf_op jit(solution)/shard_map/psum | solution.py:97
  542.3 29.9 %reduce-scatter.16.cloned.1.call-done = f32[32,128]{1,0:T(8,128)} async-done(((f32[32,1024]{1,0:T(8,128)}), f32[32,128]{1,0:T(8,128)}) %reduce-scatter.16.cloned.1.call-update) | async-done | bytes 16400 | tf_op jit(solution)/shard_map/reduce_scatter | solution.py:51
  597.5 52.0 %all-reduce.20.cloned.1.call-done = f32[32,4,2048]{2,0,1:T(8,128)} async-done(((f32[32,4,2048]{2,0,1:T(8,128)}), f32[32,4,2048]{2,0,1:T(8,128)}) %all-reduce.20.cloned.1.call-update) | async-done | bytes 1048592 | tf_op jit(solution)/shard_map/psum | solution.py:87
  659.7 40.0 %all-reduce.2 = (f32[32]{0:T(128)S(1)}, f32[32]{0:T(128)S(1)}) all-reduce(f32[32]{0:T(128)S(1)} %get-tuple-element.39, f32[32]{0:T(128)S(1)} %get-tuple-element.38), channel_id=1, replica_groups=mesh['scen'=8,'col'=4] {'scen','col'}, use_global_device_ids=true, to_apply=%region_28.29 | all-reduce | flops 64 | bytes 512 | tf_op jit(solution)/shard_map/psum | solution.py:66
  703.7 39.2 %psum.201 = f32[32]{0:T(128)S(1)} all-reduce(f32[32]{0:T(128)S(1)} %add.391), channel_id=1, replica_groups=mesh['scen'=8,'col'=4] {'scen','col'}, use_global_device_ids=true, to_apply=%region_35.36 | all-reduce | flops 32 | bytes 256 | tf_op jit(solution)/shard_map/psum | solution.py:66
  768.7 50.4 %all-reduce.22.cloned.1.call-done = f32[32,4,2048]{2,0,1:T(8,128)} async-done(((f32[32,4,2048]{2,0,1:T(8,128)}), f32[32,4,2048]{2,0,1:T(8,128)}) %all-reduce.22.cloned.1.call-update) | async-done | bytes 1048592 | tf_op jit(solution)/shard_map/psum | solution.py:87
  830.4 40.0 %psum.203 = f32[32]{0:T(128)S(1)} all-reduce(f32[32]{0:T(128)S(1)} %multiply_add_fusion.24), channel_id=1, replica_groups=mesh['scen'=8,'col'=4] {'scen','col'}, use_global_device_ids=true, to_apply=%region_40.41 | all-reduce | flops 32 | bytes 256 | tf_op jit(solution)/shard_map/psum | solution.py:97
  874.5 39.2 %psum.204 = f32[32]{0:T(128)S(1)} all-reduce(f32[32]{0:T(128)S(1)} %add.400), channel_id=1, replica_groups=mesh['scen'=8,'col'=4] {'scen','col'}, use_global_device_ids=true, to_apply=%region_44.45 | all-reduce | flops 32 | bytes 256 | tf_op jit(solution)/shard_map/psum | solution.py:66
  925.2 11.9 fusion.126
  941.0 50.3 %all-reduce.24.cloned.1.call-done = f32[32,4,2048]{2,0,1:T(8,128)} async-done(((f32[32,4,2048]{2,0,1:T(8,128)}), f32[32,4,2048]{2,0,1:T(8,128)}) %all-reduce.24.cloned.1.call-update) | async-done | bytes 1048592 | tf_op jit(solution)/shard_map/psum | solution.py:87
  992.7 40.0 %psum.206 = f32[32]{0:T(128)S(1)} all-reduce(f32[32]{0:T(128)S(1)} %multiply_add_fusion.23), channel_id=1, replica_groups=mesh['scen'=8,'col'=4] {'scen','col'}, use_global_device_ids=true, to_apply=%region_49.50 | all-reduce | flops 32 | bytes 256 | tf_op jit(solution)/shard_map/psum | solution.py:97
  1061.9 29.9 %reduce-scatter.22.cloned.1.call-done = f32[32,128]{1,0:T(8,128)} async-done(((f32[32,1024]{1,0:T(8,128)}), f32[32,128]{1,0:T(8,128)}) %reduce-scatter.22.cloned.1.call-update) | async-done | bytes 16400 | tf_op jit(solution)/shard_map/reduce_scatter | solution.py:51
  1117.1 52.0 %all-reduce.26.cloned.1.call-done = f32[32,4,2048]{2,0,1:T(8,128)} async-done(((f32[32,4,2048]{2,0,1:T(8,128)}), f32[32,4,2048]{2,0,1:T(8,128)}) %all-reduce.26.cloned.1.call-update) | async-done | bytes 1048592 | tf_op jit(solution)/shard_map/psum | solution.py:87
  1179.3 40.0 %all-reduce.1 = (f32[32]{0:T(128)S(1)}, f32[32]{0:T(128)S(1)}) all-reduce(f32[32]{0:T(128)S(1)} %get-tuple-element.25, f32[32]{0:T(128)S(1)} %get-tuple-element.24), channel_id=1, replica_groups=mesh['scen'=8,'col'=4] {'scen','col'}, use_global_device_ids=true, to_apply=%region_53.54 | all-reduce | flops 64 | bytes 512 | tf_op jit(solution)/shard_map/psum | solution.py:66
  1223.3 39.2 %psum.210 = f32[32]{0:T(128)S(1)} all-reduce(f32[32]{0:T(128)S(1)} %add.420), channel_id=1, replica_groups=mesh['scen'=8,'col'=4] {'scen','col'}, use_global_device_ids=true, to_apply=%region_60.61 | all-reduce | flops 32 | bytes 256 | tf_op jit(solution)/shard_map/psum | solution.py:66
  1272.5 11.9 fusion.122
  1288.4 50.4 %all-reduce.28.cloned.1.call-done = f32[32,4,2048]{2,0,1:T(8,128)} async-done(((f32[32,4,2048]{2,0,1:T(8,128)}), f32[32,4,2048]{2,0,1:T(8,128)}) %all-reduce.28.cloned.1.call-update) | async-done | bytes 1048592 | tf_op jit(solution)/shard_map/psum | solution.py:87
  1350.1 40.0 %psum.212 = f32[32]{0:T(128)S(1)} all-reduce(f32[32]{0:T(128)S(1)} %multiply_add_fusion.21), channel_id=1, replica_groups=mesh['scen'=8,'col'=4] {'scen','col'}, use_global_device_ids=true, to_apply=%region_65.66 | all-reduce | flops 32 | bytes 256 | tf_op jit(solution)/shard_map/psum | solution.py:97
  1394.2 39.2 %psum.213 = f32[32]{0:T(128)S(1)} all-reduce(f32[32]{0:T(128)S(1)} %add.429), channel_id=1, replica_groups=mesh['scen'=8,'col'=4] {'scen','col'}, use_global_device_ids=true, to_apply=%region_69.70 | all-reduce | flops 32 | bytes 256 | tf_op jit(solution)/shard_map/psum | solution.py:66
  1445.3 11.9 fusion.120
  1462.7 48.7 %all-reduce.30.cloned.1.call-done = f32[32,4,2048]{2,0,1:T(8,128)} async-done(((f32[32,4,2048]{2,0,1:T(8,128)}), f32[32,4,2048]{2,0,1:T(8,128)}) %all-reduce.30.cloned.1.call-update) | async-done | bytes 1048592 | tf_op jit(solution)/shard_map/psum | solution.py:87
  1514.0 40.1 %psum.215 = f32[32]{0:T(128)} all-reduce(f32[32]{0:T(128)} %multiply_add_fusion.20), channel_id=1, replica_groups=mesh['scen'=8,'col'=4] {'scen','col'}, use_global_device_ids=true, to_apply=%region_74.75 | all-reduce | flops 32 | bytes 256 | tf_op jit(solution)/shard_map/psum | solution.py:97
  (292 shorter events, 374.7 us)
Async XLA Ops:
  7.2 47.4 %reduce-scatter.10.cloned.1.call-start = ((), (), s32[]{:S(2)}) async-start(), calls=%async_computation.9 | async-start | bytes 147456 | tf_op jit(solution)/shard_map/reduce_scatter | solution.py:51
  18.1 113.7 %all-reduce.14.cloned.1.call-start = ((), (), s32[]{:S(2)}) async-start(), calls=%async_computation.10 | async-start | bytes 2097152 | tf_op jit(solution)/shard_map/psum | solution.py:87
  18.9 1243.5 %copy-start.43 = (f32[128]{0:T(128)}, f32[128]{0:T(128)S(1)}, u32[]{:S(2)}) copy-start(f32[128]{0:T(128)S(1)} %dynamic_slice.9) | copy-start | bytes 1540
  22.1 225.1 %copy-start.24 = (f32[32,4,256]{2,0,1:T(8,128)}, f32[32,4,256]{2,0,1:T(8,128)S(1)}, u32[]{:S(2)}) copy-start(f32[32,4,256]{2,0,1:T(8,128)S(1)} %get-tuple-element.60) | copy-start | bytes 393220
  79.8 105.3 %reduce-scatter.12.cloned.1.call-start = ((), (), s32[]{:S(2)}) async-start(), calls=%async_computation.11 | async-start | bytes 147456 | tf_op jit(solution)/shard_map/reduce_scatter | solution.py:51
  141.7 159.7 %all-reduce.16.cloned.1.call-start = ((), (), s32[]{:S(2)}) async-start(), calls=%async_computation.12 | async-start | bytes 2097152 | tf_op jit(solution)/shard_map/psum | solution.py:87
  181.9 332.5 %copy-start.49 = (f32[32]{0:T(128)}, f32[32]{0:T(128)S(1)}, u32[]{:S(2)}) copy-start(f32[32]{0:T(128)S(1)} %div.54) | copy-start | bytes 388
  251.0 104.9 %reduce-scatter.14.cloned.1.call-start = ((), (), s32[]{:S(2)}) async-start(), calls=%async_computation.13 | async-start | bytes 147456 | tf_op jit(solution)/shard_map/reduce_scatter | solution.py:51
  312.7 160.3 %all-reduce.18.cloned.1.call-start = ((), (), s32[]{:S(2)}) async-start(), calls=%async_computation.14 | async-start | bytes 2097152 | tf_op jit(solution)/shard_map/psum | solution.py:87
  352.7 161.8 %copy-start.46 = (f32[32]{0:T(128)}, f32[32]{0:T(128)S(1)}, u32[]{:S(2)}) copy-start(f32[32]{0:T(128)S(1)} %div.56) | copy-start | bytes 388
  422.5 149.7 %reduce-scatter.16.cloned.1.call-start = ((), (), s32[]{:S(2)}) async-start(), calls=%async_computation.15 | async-start | bytes 147456 | tf_op jit(solution)/shard_map/reduce_scatter | solution.py:51
  422.7 618.7 %copy-start.44 = (f32[4,2048]{1,0:T(4,128)}, f32[4,2048]{1,0:T(4,128)S(1)}, u32[]{:S(2)}) copy-start(f32[4,2048]{1,0:T(4,128)S(1)} %broadcast_subtract_fusion) | copy-start | bytes 98308
  474.5 570.3 %copy-start.35 = (f32[4,2048]{1,0:T(4,128)}, f32[4,2048]{1,0:T(4,128)S(1)}, u32[]{:S(2)}) copy-start(f32[4,2048]{1,0:T(4,128)S(1)} %pad_convert_fusion) | copy-start | bytes 98308
  539.1 110.4 %all-reduce.20.cloned.1.call-start = ((), (), s32[]{:S(2)}) async-start(), calls=%async_computation.16 | async-start | bytes 2097152 | tf_op jit(solution)/shard_map/psum | solution.py:87
  542.3 222.6 %copy-start.25 = (f32[32,4,256]{2,0,1:T(8,128)}, f32[32,4,256]{2,0,1:T(8,128)S(1)}, u32[]{:S(2)}) copy-start(f32[32,4,256]{2,0,1:T(8,128)S(1)} %get-tuple-element.70) | copy-start | bytes 393220
  597.5 105.3 %reduce-scatter.18.cloned.1.call-start = ((), (), s32[]{:S(2)}) async-start(), calls=%async_computation.17 | async-start | bytes 147456 | tf_op jit(solution)/shard_map/reduce_scatter | solution.py:51
  659.4 159.7 %all-reduce.22.cloned.1.call-start = ((), (), s32[]{:S(2)}) async-start(), calls=%async_computation.18 | async-start | bytes 2097152 | tf_op jit(solution)/shard_map/psum | solution.py:87
  699.6 333.1 %copy-start.50 = (f32[32]{0:T(128)}, f32[32]{0:T(128)S(1)}, u32[]{:S(2)}) copy-start(f32[32]{0:T(128)S(1)} %div.60) | copy-start | bytes 388
  743.0 170.6 %copy-start.33 = (f32[32,128]{1,0:T(8,128)}, f32[32,128]{1,0:T(8,128)S(1)}, u32[]{:S(2)}) copy-start(f32[32,128]{1,0:T(8,128)S(1)} %get-tuple-element.35) | copy-start | bytes 49156
  768.6 104.9 %reduce-scatter.20.cloned.1.call-start = ((), (), s32[]{:S(2)}) async-start(), calls=%async_computation.19 | async-start | bytes 147456 | tf_op jit(solution)/shard_map/reduce_scatter | solution.py:51
  830.4 160.9 %all-reduce.24.cloned.1.call-start = ((), (), s32[]{:S(2)}) async-start(), calls=%async_computation.20 | async-start | bytes 2097152 | tf_op jit(solution)/shard_map/psum | solution.py:87
  870.4 162.3 %copy-start.47 = (f32[32]{0:T(128)}, f32[32]{0:T(128)S(1)}, u32[]{:S(2)}) copy-start(f32[32]{0:T(128)S(1)} %div.62) | copy-start | bytes 388
  940.8 151.0 %reduce-scatter.22.cloned.1.call-start = ((), (), s32[]{:S(2)}) async-start(), calls=%async_computation.21 | async-start | bytes 147456 | tf_op jit(solution)/shard_map/reduce_scatter | solution.py:51
  1058.7 110.4 %all-reduce.26.cloned.1.call-start = ((), (), s32[]{:S(2)}) async-start(), calls=%async_computation.22 | async-start | bytes 2097152 | tf_op jit(solution)/shard_map/psum | solution.py:87
  1061.9 222.6 %copy-start.26 = (f32[32,4,256]{2,0,1:T(8,128)}, f32[32,4,256]{2,0,1:T(8,128)S(1)}, u32[]{:S(2)}) copy-start(f32[32,4,256]{2,0,1:T(8,128)S(1)} %get-tuple-element.78) | copy-start | bytes 393220
  1117.1 105.3 %reduce-scatter.24.cloned.1.call-start = ((), (), s32[]{:S(2)}) async-start(), calls=%async_computation.23 | async-start | bytes 147456 | tf_op jit(solution)/shard_map/reduce_scatter | solution.py:51
  1179.0 159.8 %all-reduce.28.cloned.1.call-start = ((), (), s32[]{:S(2)}) async-start(), calls=%async_computation.24 | async-start | bytes 2097152 | tf_op jit(solution)/shard_map/psum | solution.py:87
  1262.6 170.7 %copy-start.34 = (f32[32,128]{1,0:T(8,128)}, f32[32,128]{1,0:T(8,128)S(1)}, u32[]{:S(2)}) copy-start(f32[32,128]{1,0:T(8,128)S(1)} %get-tuple-element.21) | copy-start | bytes 49156
  1288.3 104.9 %reduce-scatter.26.cloned.1.call-start = ((), (), s32[]{:S(2)}) async-start(), calls=%async_computation.25 | async-start | bytes 147456 | tf_op jit(solution)/shard_map/reduce_scatter | solution.py:51
  1350.1 161.3 %all-reduce.30.cloned.1.call-start = ((), (), s32[]{:S(2)}) async-start(), calls=%async_computation.26 | async-start | bytes 2097152 | tf_op jit(solution)/shard_map/psum | solution.py:87
  1460.9 107.2 %copy-start.15 = (f32[32,4,2048]{2,0,1:T(8,128)S(1)}, f32[32,4,2048]{2,0,1:T(8,128)}, u32[]{:S(2)}) copy-start(f32[32,4,2048]{2,0,1:T(8,128)} %all-reduce.26.cloned.1.call-done) | copy-start | bytes 3145732
  1460.9 107.2 %copy-start.19 = (f32[32,4,2048]{2,0,1:T(8,128)S(1)}, f32[32,4,2048]{2,0,1:T(8,128)}, u32[]{:S(2)}) copy-start(f32[32,4,2048]{2,0,1:T(8,128)} %all-reduce.28.cloned.1.call-done) | copy-start | bytes 3145732
  (44 other events, 1123.3 us)
Sparse Core Ops, SparseCore 0:
  18.2 36.2 reduce-scatter.9
  79.9 51.8 all-reduce.13
  141.8 32.8 reduce-scatter.11
  251.1 50.3 all-reduce.15
  312.8 32.8 reduce-scatter.13
  422.6 50.3 all-reduce.17
  539.2 32.8 reduce-scatter.15
  597.6 51.8 all-reduce.19
  659.5 32.8 reduce-scatter.17
  768.7 50.3 all-reduce.21
  830.5 32.8 reduce-scatter.19
  940.9 50.3 all-reduce.23
  1058.9 32.8 reduce-scatter.21
  1117.2 51.8 all-reduce.25
  1179.1 32.8 reduce-scatter.23
  1288.4 50.3 all-reduce.27
  1350.2 32.8 reduce-scatter.25
  1461.0 50.3 all-reduce.29
where the time goes:
time: 1610 us; the launch traced here: 1590 us
  blocking collectives  692 us (43%)
  waiting for transfers between devices  549 us (34%)
  matrix products  292 us (18%)
  other arithmetic  39.5 us (2%)
    psum x9, waiting for transfers between devices, body(): lax.psum(forward_partial_value + jnp.einsum('bsk,smk->bsm', dir_second.as...  456 us
    psum x9, blocking collectives, total_norm(): return lax.psum(local_squares(first_vec, second_vec), ('scen', 'col'))  355 us
    psum x6, blocking collectives, body(): curv = lax.psum(curv_term, ('scen', 'col'))  240 us
    dot_general x9, matrix products, body(): lax.dot_general(dir_first_bf, tech_flat, (((1,), (1,)), ((), ())), prefer...  107 us
    reduce_scatter x9, waiting for transfers between devices, couple(): lax.psum_scatter(partial_value, 'scen', scatter_dimension=1, tiled=True)  92.3 us
    dot_general x9, matrix products, adjoint(): jnp.dot(rows_bf.reshape(batch, scen_local * rows), tech_flat, preferred_e...  87.1 us
    all_gather x9, blocking collectives, body(): lax.all_gather(dir_first.astype(bf16), 'scen', axis=1, tiled=True)  86.4 us
  transfers between devices with their start and end apart: 18, of which 12 were waited for; matrix products, arithmetic and copies ran while one was open for 2% of the time, Pallas kernels for 0%

commit v1 on v0

--- a/solution.py
+++ b/solution.py
@@ -1,6 +1,10 @@
+import functools
+
 import jax
 import jax.numpy as jnp
 from jax import lax
+from jax.experimental import pallas as pl
+from jax.experimental.pallas import tpu as pltpu
 from jax.sharding import PartitionSpec as P
 
 NCONE = 128
@@ -125,6 +129,470 @@
     return (first_out, second_sol, slack_out, dual_out)
 
 
+def kernel_body(
+    dims,
+    tech_hbm, rec_hbm, rhs_hbm, cost1, cost2, cid, starts,
+    x_out, y_out, slack_out, dual_out,
+    tech, rec, g, dual, slack, onehot, q_all, part, rsc, q_own,
+    acc, rs1, ag1, back2, res2, dir2, res1, dir1,
+    nrm_own, nrm1, nrm_mid, nrm2, crv_own, crv1, crv_mid, crv2,
+    nres, ratio, alpha, qq, xs,
+    ld_t, ld_r, ld_g,
+    ag1_s, ag1_r, n1_s, n1_r, n2_s, n2_r, rsc_s, rsc_r, agc_s, agc_r,
+    c1_s, c1_r, c2_s, c2_r, rs1_s, rs1_r, fin_s, fin_r,
+):
+    n_scen, n_col, B, S, R, C1, C2 = dims
+    f32, bf16 = jnp.float32, jnp.bfloat16
+    RQ = R // n_col
+    SH = C1 // n_scen
+    G = B // 8
+    W = 128 // G
+    LAG = min(2, S)
+    ms = lax.axis_index("scen")
+    mc = lax.axis_index("col")
+
+    def scen_peer(j):
+        return lax.rem(ms + j, n_scen)
+
+    def col_peer(j):
+        return lax.rem(mc + j, n_col)
+
+    def to_scen(src, dst, ss, rs, j):
+        return pltpu.make_async_remote_copy(
+            src_ref=src, dst_ref=dst, send_sem=ss, recv_sem=rs,
+            device_id=(scen_peer(j), mc), device_id_type=pl.DeviceIdType.MESH)
+
+    def to_col(src, dst, ss, rs, j):
+        return pltpu.make_async_remote_copy(
+            src_ref=src, dst_ref=dst, send_sem=ss, recv_sem=rs,
+            device_id=(ms, col_peer(j)), device_id_type=pl.DeviceIdType.MESH)
+
+    SJ = range(1, n_scen)
+    CJ = range(1, n_col)
+
+    def d_ag1(j):
+        return to_scen(ag1.at[ms], ag1.at[ms], ag1_s.at[j - 1], ag1_r.at[j - 1], j)
+
+    def d_n1(j):
+        return to_scen(nrm_own, nrm1.at[j - 1], n1_s.at[j - 1], n1_r.at[j - 1], j)
+
+    def d_n2(j):
+        return to_col(nrm_mid, nrm2.at[j - 1], n2_s.at[j - 1], n2_r.at[j - 1], j)
+
+    def d_rsc(j, s):
+        return to_col(part.at[s, col_peer(j)], rsc.at[j - 1, s], rsc_s.at[j - 1, s], rsc_r.at[j - 1, s], j)
+
+    def d_agc(j, s):
+        return to_col(q_all.at[s, mc], q_all.at[s, mc], agc_s.at[j - 1, s], agc_r.at[j - 1, s], j)
+
+    def d_c1(j):
+        return to_col(crv_own, crv1.at[j - 1], c1_s.at[j - 1], c1_r.at[j - 1], j)
+
+    def d_c2(j):
+        return to_scen(crv_mid, crv2.at[j - 1], c2_s.at[j - 1], c2_r.at[j - 1], j)
+
+    def d_rs1(j):
+        return to_scen(acc.at[scen_peer(j)], rs1.at[j - 1], rs1_s.at[j - 1], rs1_r.at[j - 1], j)
+
+    def d_fin(j):
+        return to_scen(xs.at[ms], xs.at[ms], fin_s.at[j - 1], fin_r.at[j - 1], j)
+
+    group = lax.broadcasted_iota(jnp.int32, (8, 128), 1) // W
+
+    def pack(x):
+        shift = 64
+        while shift >= W:
+            x = x + pltpu.roll(x, shift, 1)
+            shift //= 2
+        out = x[0:8]
+        for k in range(1, G):
+            out = jnp.where(group == k, x[8 * k:8 * k + 8], out)
+        return out
+
+    def unpack(p):
+        return jnp.concatenate(
+            [jnp.broadcast_to(jnp.sum(jnp.where(group == k, p, 0.0), axis=1, keepdims=True), (8, 128))
+             for k in range(G)], axis=0)
+
+    def lanes(x):
+        out = x[:, 0:128]
+        for k in range(1, x.shape[1] // 128):
+            out = out + x[:, 128 * k:128 * k + 128]
+        return out
+
+    def load_t(s):
+        return pltpu.make_async_copy(tech_hbm.at[s], tech.at[s], ld_t.at[s])
+
+    def load_r(s):
+        return pltpu.make_async_copy(rec_hbm.at[s], rec.at[s], ld_r.at[s])
+
+    load_g = pltpu.make_async_copy(rhs_hbm, g, ld_g)
+    load_g.start()
+    for s in range(S):
+        load_t(s).start()
+        load_r(s).start()
+
+    barrier = pltpu.get_barrier_semaphore()
+    for j in SJ:
+        pl.semaphore_signal(barrier, inc=1, device_id=(scen_peer(j), mc), device_id_type=pl.DeviceIdType.MESH)
+    for j in CJ:
+        pl.semaphore_signal(barrier, inc=1, device_id=(ms, col_peer(j)), device_id_type=pl.DeviceIdType.MESH)
+
+    dir1[...] = jnp.zeros_like(dir1)
+    dir2[...] = jnp.zeros_like(dir2)
+    q_own[...] = jnp.zeros_like(q_own)
+    dual[...] = jnp.zeros_like(dual)
+    xs[ms] = jnp.zeros((B, SH), f32)
+    y_out[...] = jnp.zeros_like(y_out)
+    load_g.wait()
+
+    def init(s, c):
+        ids = cid[s]
+        onehot[s] = (lax.broadcasted_iota(jnp.int32, (NCONE, R), 0) == ids).astype(f32).astype(bf16)
+        for k in range(n_col):
+            q_all[s, k] = g[s, :, k * RQ:(k + 1) * RQ].astype(bf16)
+        return c
+
+    lax.fori_loop(0, S, init, 0)
+    pl.semaphore_wait(barrier, n_scen + n_col - 2)
+
+    def curv_forward():
+        total = crv_own[...]
+        for j in CJ:
+            d_c1(j).wait_recv()
+            total = total + crv1[j - 1]
+        for j in CJ:
+            d_c1(j).wait_send()
+        crv_mid[...] = total
+        for j in SJ:
+            d_c2(j).start()
+
+    def curv_finish():
+        total = crv_mid[...]
+        for j in SJ:
+            d_c2(j).wait_recv()
+            total = total + crv2[j - 1]
+        for j in SJ:
+            d_c2(j).wait_send()
+        alpha[...] = nres[...] / unpack(total)
+
+    def advance():
+        a = alpha[...][:, 0:1]
+        xs[ms] = xs[ms] + a * dir1[...]
+
+        def one(s, c):
+            y_out[s] = y_out[s] + a * dir2[s]
+            for k in range(n_col):
+                cols = slice(k * RQ, (k + 1) * RQ)
+                g[s, :, cols] = g[s, :, cols] - a * q_all[s, k].astype(f32)
+            return c
+
+        lax.fori_loop(0, S, one, 0)
+
+    def split(x):
+        hi = x.astype(bf16)
+        return [hi, (x - hi.astype(f32)).astype(bf16)]
+
+    def project(s, c):
+        st = starts[s]
+        v = g[s] - dual[s]
+        lead_v = v * st
+        tail_v = v * v * (1.0 - st)
+        stack = jnp.concatenate(split(lead_v) + split(tail_v), axis=0)
+        sums = lax.dot_general(stack, onehot[s], (((1,), (1,)), ((), ())), preferred_element_type=f32)
+        lead = sums[0:B] + sums[B:2 * B]
+        tail = sums[2 * B:3 * B] + sums[3 * B:4 * B]
+        head, scale = cone_factors(lead, tail)
+        stack2 = jnp.concatenate(split(head) + split(scale), axis=0)
+        outs = jnp.dot(stack2, onehot[s], preferred_element_type=f32)
+        head_rows = outs[0:B] + outs[B:2 * B]
+        scale_rows = outs[2 * B:3 * B] + outs[3 * B:4 * B]
+        sl = st * head_rows + (1.0 - st) * v * scale_rows
+        du = sl - v
+        slack[s] = sl
+        dual[s] = du
+        d = g[s] - sl - du
+        for k in range(n_col):
+            q_all[s, k] = d[:, k * RQ:(k + 1) * RQ].astype(bf16)
+        return c
+
+    def step_body(t, carry):
+        step = lax.rem(t, CG_STEPS)
+        acc[...] = jnp.zeros_like(acc)
+
+        def back(s, c):
+            @pl.when(t == 0)
+            def _():
+                load_t(s).wait()
+                load_r(s).wait()
+
+            @pl.when(step != 0)
+            def _():
+                for j in CJ:
+                    d_agc(j, s).wait_recv()
+                for j in CJ:
+                    d_agc(j, s).wait_send()
+
+            z = jnp.concatenate([q_all[s, k] for k in range(n_col)], axis=1)
+            f = jnp.dot(z, tech[s], preferred_element_type=f32)
+            for i in range(n_scen):
+                acc[i] = acc[i] + f[:, i * SH:(i + 1) * SH]
+            back2[s] = jnp.dot(z, rec[s], preferred_element_type=f32)
+
+            @pl.when(jnp.logical_and(step != 0, s == S - 1))
+            def _():
+                curv_forward()
+
+            return c
+
+        lax.fori_loop(0, S, back, 0)
+        for j in SJ:
+            d_rs1(j).start()
+
+        @pl.when(step != 0)
+        def _():
+            curv_finish()
+
+        tot = acc[ms]
+        for j in SJ:
+            d_rs1(j).wait_recv()
+            tot = tot + rs1[j - 1]
+        for j in SJ:
+            d_rs1(j).wait_send()
+
+        @pl.when(step == 0)
+        def _():
+            res1[...] = tot - cost1[:, pl.ds(pl.multiple_of(ms * SH, 128), SH)]
+            for s in range(S):
+                res2[s] = back2[s] - cost2[s]
+
+        @pl.when(step != 0)
+        def _():
+            a = alpha[...][:, 0:1]
+            res1[...] = res1[...] - a * (dir1[...] + tot)
+            for s in range(S):
+                res2[s] = res2[s] - a * (dir2[s] + back2[s])
+
+        r1 = res1[...]
+        ag1[ms] = r1.astype(bf16)
+        for j in SJ:
+            d_ag1(j).start()
+        sq = lanes(r1 * r1)
+        for s in range(S):
+            r2 = res2[s]
+            sq = sq + lanes(r2 * r2)
+        nrm_own[...] = pack(sq)
+        for j in SJ:
+            d_n1(j).start()
+
+        @pl.when(step != 0)
+        def _():
+            advance()
+
+        for j in SJ:
+            d_ag1(j).wait_recv()
+        for j in SJ:
+            d_ag1(j).wait_send()
+
+        def norm_forward():
+            total = nrm_own[...]
+            for j in SJ:
+                d_n1(j).wait_recv()
+                total = total + nrm1[j - 1]
+            for j in SJ:
+                d_n1(j).wait_send()
+            nrm_mid[...] = total
+            for j in CJ:
+                d_n2(j).start()
+
+        def norm_finish():
+            total = nrm_mid[...]
+            for j in CJ:
+                d_n2(j).wait_recv()
+                total = total + nrm2[j - 1]
+            for j in CJ:
+                d_n2(j).wait_send()
+            new = unpack(total)
+
+            @pl.when(step == 0)
+            def _():
+                ratio[...] = jnp.zeros_like(ratio)
+
+            @pl.when(step != 0)
+            def _():
+                ratio[...] = new / nres[...]
+
+            nres[...] = new
+            r = ratio[...][:, 0:1]
+            d1 = res1[...] + r * dir1[...]
+            dir1[...] = d1
+            dsq = lanes(d1 * d1)
+            for s in range(S):
+                d2 = res2[s] + r * dir2[s]
+                dir2[s] = d2
+                dsq = dsq + lanes(d2 * d2)
+            qq[...] = dsq
+
+        def process(s):
+            r = ratio[...][:, 0:1]
+            q = part[s, mc].astype(f32)
+            for j in CJ:
+                d_rsc(j, s).wait_recv()
+                q = q + rsc[j - 1, s].astype(f32)
+            q = q + r * q_own[s]
+            q_own[s] = q
+            q_all[s, mc] = q.astype(bf16)
+            for j in CJ:
+                d_agc(j, s).start()
+            qq[...] = qq[...] + lanes(q * q)
+
+        def front(s, c):
+            x = jnp.concatenate([ag1[i] for i in range(n_scen)], axis=1)
+            y = res2[s].astype(bf16)
+            dn = (((1,), (1,)), ((), ()))
+            for k in range(n_col):
+                rows = pl.ds(k * RQ, RQ)
+                p = lax.dot_general(x, tech[s, rows, :], dn, preferred_element_type=f32)
+                p = p + lax.dot_general(y, rec[s, rows, :], dn, preferred_element_type=f32)
+                part[s, k] = p.astype(bf16)
+            for j in CJ:
+                d_rsc(j, s).start()
+
+            @pl.when(s == 0)
+            def _():
+                norm_forward()
+
+            @pl.when(s == LAG - 1)
+            def _():
+                norm_finish()
+
+            @pl.when(s >= LAG)
+            def _():
+                process(s - LAG)
+
+            return c
+
+        lax.fori_loop(0, S, front, 0)
+
+        def drain(s, c):
+            process(s)
+            return c
+
+        lax.fori_loop(S - LAG, S, drain, 0)
+        crv_own[...] = pack(qq[...])
+        for j in CJ:
+            d_c1(j).start()
+        for s in range(S):
+            for j in CJ:
+                d_rsc(j, s).wait_send()
+
+        @pl.when(step == CG_STEPS - 1)
+        def _():
+            curv_forward()
+
+            def arrive(s, c):
+                for j in CJ:
+                    d_agc(j, s).wait_recv()
+                for j in CJ:
+                    d_agc(j, s).wait_send()
+                return c
+
+            lax.fori_loop(0, S, arrive, 0)
+            curv_finish()
+            advance()
+            lax.fori_loop(0, S, project, 0)
+
+        return carry
+
+    lax.fori_loop(0, ITERS * CG_STEPS, step_body, 0)
+
+    for j in SJ:
+        d_fin(j).start()
+    here = pl.ds(pl.multiple_of(mc * RQ, 128), RQ)
+    for s in range(S):
+        slack_out[s] = slack[s, :, here]
+        dual_out[s] = dual[s, :, here]
+    for j in SJ:
+        d_fin(j).wait_recv()
+    for j in SJ:
+        d_fin(j).wait_send()
+    for i in range(n_scen):
+        x_out[:, i * SH:(i + 1) * SH] = xs[i]
+
+
+def fused(tech, recourse, rhs, cost_first, cost_second, cone_id):
+    f32, bf16 = jnp.float32, jnp.bfloat16
+    n_scen = lax.axis_size("scen")
+    n_col = lax.axis_size("col")
+    B = rhs.shape[0]
+    S, R, C1 = tech.shape
+    C2 = recourse.shape[2]
+    RQ = R // n_col
+    SH = C1 // n_scen
+    starts = jnp.concatenate(
+        [jnp.ones((S, 1), f32), (cone_id[:, 1:] != cone_id[:, :-1]).astype(f32)], axis=1)
+    vm = pl.BlockSpec(memory_space=pltpu.VMEM)
+    hbm = pl.BlockSpec(memory_space=pl.ANY)
+    V = pltpu.VMEM
+    D = pltpu.SemaphoreType.DMA
+    ns, nc = n_scen - 1, n_col - 1
+    scratch = [
+        V((S, R, C1), bf16), V((S, R, C2), bf16),
+        V((S, B, R), f32), V((S, B, R), f32), V((S, B, R), f32),
+        V((S, NCONE, R), bf16),
+        V((S, n_col, B, RQ), bf16), V((S, n_col, B, RQ), bf16), V((nc, S, B, RQ), bf16),
+        V((S, B, RQ), f32),
+        V((n_scen, B, SH), f32), V((ns, B, SH), f32), V((n_scen, B, SH), bf16),
+        V((S, B, C2), f32), V((S, B, C2), f32), V((S, B, C2), f32),
+        V((B, SH), f32), V((B, SH), f32),
+        V((8, 128), f32), V((ns, 8, 128), f32), V((8, 128), f32), V((nc, 8, 128), f32),
+        V((8, 128), f32), V((nc, 8, 128), f32), V((8, 128), f32), V((ns, 8, 128), f32),
+        V((B, 128), f32), V((B, 128), f32), V((B, 128), f32), V((B, 128), f32),
+        V((n_scen, B, SH), f32),
+        D((S,)), D((S,)), D,
+        D((ns,)), D((ns,)), D((ns,)), D((ns,)), D((nc,)), D((nc,)),
+        D((nc, S)), D((nc, S)), D((nc, S)), D((nc, S)),
+        D((nc,)), D((nc,)), D((ns,)), D((ns,)), D((ns,)), D((ns,)), D((ns,)), D((ns,)),
+    ]
+    x, y, slack, dual = pl.pallas_call(
+        functools.partial(kernel_body, (n_scen, n_col, B, S, R, C1, C2)),
+        out_shape=(
+            jax.ShapeDtypeStruct((B, C1), f32),
+            jax.ShapeDtypeStruct((S, B, C2), f32),
+            jax.ShapeDtypeStruct((S, B, RQ), f32),
+            jax.ShapeDtypeStruct((S, B, RQ), f32),
+        ),
+        in_specs=[hbm, hbm, hbm, vm, vm, vm, vm],
+        out_specs=(vm, vm, vm, vm),
+        scratch_shapes=scratch,
+        compiler_params=pltpu.CompilerParams(
+            collective_id=0, has_side_effects=True, vmem_limit_bytes=58 * 1024 * 1024),
+    )(
+        tech, recourse, jnp.transpose(rhs, (1, 0, 2)),
+        cost_first.reshape(1, C1), cost_second.reshape(S, 1, C2),
+        cone_id.reshape(S, 1, R), starts.reshape(S, 1, R),
+    )
+    back = lambda a: jnp.transpose(a, (1, 0, 2))
+    return x, back(y), back(slack), back(dual)
+
+
+def program(tech, recourse, rhs, cost_first, cost_second, cone_id):
+    n_scen = lax.axis_size("scen")
+    n_col = lax.axis_size("col")
+    batch = rhs.shape[0]
+    fits = (
+        tech.shape[2] % (128 * n_scen) == 0
+        and tech.shape[1] % (128 * n_col) == 0
+        and recourse.shape[2] % 128 == 0
+        and batch % 16 == 0
+        and 1024 % batch == 0
+        and n_scen > 1
+        and n_col > 1
+    )
+    run = fused if fits else body
+    return run(tech, recourse, rhs, cost_first, cost_second, cone_id)
+
+
 def solution(mesh):
     placed = (
         P("scen", None, "col"),
@@ -135,7 +603,7 @@
         P("scen", None),
     )
     return jax.shard_map(
-        body,
+        program,
         mesh=mesh,
         in_specs=placed,
         out_specs=(

time: 1610 us -> 383 us (0.24); the launches traced: 1590 us -> 383 us
  blocking collectives: 692 us -> 0 us
  waiting for transfers between devices: 549 us -> 0 us
  Pallas kernels: 0 us -> 368 us
  matrix products: 292 us -> 0 us
  other arithmetic: 39.5 us -> 1 us
    psum x15 -> x0, blocking collectives: 595 us -> none  [the longest x9 355 us: total_norm(): return lax.psum(local_squares(first_vec, second_vec), ('scen', 'col'))]
    psum x9 -> x0, waiting for transfers between devices: 456 us -> none  [body(): lax.psum(forward_partial_value + jnp.einsum('bsk,smk->bsm', dir_second.as...]
    pallas_call x0 -> x1, Pallas kernels: none -> 368 us  [fused(): pl.pallas_call(functools.partial(kernel_body, (n_scen, n_col, B, S, R, C1...]
    dot_general x48 -> x0, matrix products: 292 us -> none  [the longest x9 107 us: body(): lax.dot_general(dir_first_bf, tech_flat, (((1,), (1,)), ((), ())), prefer...]
    all_gather x10 -> x0, blocking collectives: 96.7 us -> none  [the longest x9 86.4 us: body(): lax.all_gather(dir_first.astype(bf16), 'scen', axis=1, tiled=True)]
    reduce_scatter x9 -> x0, waiting for transfers between devices: 92.3 us -> none  [couple(): lax.psum_scatter(partial_value, 'scen', scatter_dimension=1, tiled=True)]
    reduce_sum x30 -> x0, other arithmetic: 23.6 us -> none  [the longest x15 11.8 us: local_squares(): jnp.sum(first_vec * first_vec, axis=1)]
  transfers between devices with their start and end apart: 18 -> 0, of which waited for: 12 -> 0; matrix products, arithmetic and copies ran while one was open for 2% -> 0% of each run, Pallas kernels for 0% -> 0%
where the time goes in v1:
time: 383 us
  Pallas kernels  368 us (96%)
  local copies, waits for them, and re-layouts  13 us (3%)
    pallas_call x1, Pallas kernels, fused(): pl.pallas_call(functools.partial(kernel_body, (n_scen, n_col, B, S, R, C1...  368 us
    unnamed x5, local copies, waits for them, and re-layouts  9.68 us

profile of v1, /device:TPU:0, one launch (start us, length us, event | category | flops | bytes accessed | tf_op | source)
XLA Modules:
  0.0 382.5 jit_solution(3874611934049759600)
XLA Ops:
  0.6 1.3 reshape.23.cost2
  1.9 0.9 slice_compare_fusion
  2.8 0.1 pad_convert_fusion
  2.9 0.6 reshape.28.starts
  3.6 1.4 reshape.24.cid
  5.0 2.8 copy.15
  7.8 367.9 %shard_map.93 = (f32[32,1024]{1,0:T(8,128)}, f32[4,32,256]{2,1,0:T(8,128)}, f32[4,32,512]{2,1,0:T(8,128)}, f32[4,32,512]{2,1,0:T(8,128)}) custom-call(bf16[4,2048,1024]{2,1,0:T(8,128)(2,1)} %tech_hbm.1, bf16[4,2048,256]{2,1,0:T(8,128)(2,1)} %rec_hbm.1, f32[4,32,2048]{2,1,0:T(8,128)} %bitcast.7, f32[1,1024]{1,0:T(1,128)} %bitcast.11, ...), custom_call_target="tpu_custom_call" | custom-call | tf_op jit(solution)/shard_map/pallas_call | solution.py:557
  375.7 1.6 copy.11
  377.3 1.8 copy.12
  379.1 1.8 copy.13
  381.0 1.6 copy.17

commit v2 on v1

--- a/solution.py
+++ b/solution.py
@@ -134,7 +134,7 @@
     tech_hbm, rec_hbm, rhs_hbm, cost1, cost2, cid, starts,
     x_out, y_out, slack_out, dual_out,
     tech, rec, g, dual, slack, onehot, q_all, part, rsc, q_own,
-    acc, rs1, ag1, back2, res2, dir2, res1, dir1,
+    acc, snd, rs1, ag1, back2, res2, dir2, res1, dir1,
     nrm_own, nrm1, nrm_mid, nrm2, crv_own, crv1, crv_mid, crv2,
     nres, ratio, alpha, qq, xs,
     ld_t, ld_r, ld_g,
@@ -147,7 +147,6 @@
     SH = C1 // n_scen
     G = B // 8
     W = 128 // G
-    LAG = min(2, S)
     ms = lax.axis_index("scen")
     mc = lax.axis_index("col")
 
@@ -192,7 +191,7 @@
         return to_scen(crv_mid, crv2.at[j - 1], c2_s.at[j - 1], c2_r.at[j - 1], j)
 
     def d_rs1(j):
-        return to_scen(acc.at[scen_peer(j)], rs1.at[j - 1], rs1_s.at[j - 1], rs1_r.at[j - 1], j)
+        return to_scen(snd.at[scen_peer(j)], rs1.at[j - 1], rs1_s.at[j - 1], rs1_r.at[j - 1], j)
 
     def d_fin(j):
         return to_scen(xs.at[ms], xs.at[ms], fin_s.at[j - 1], fin_r.at[j - 1], j)
@@ -247,7 +246,7 @@
     load_g.wait()
 
     def init(s, c):
-        ids = cid[s]
+        ids = cid[pl.ds(s, 1), :]
         onehot[s] = (lax.broadcasted_iota(jnp.int32, (NCONE, R), 0) == ids).astype(f32).astype(bf16)
         for k in range(n_col):
             q_all[s, k] = g[s, :, k * RQ:(k + 1) * RQ].astype(bf16)
@@ -294,7 +293,7 @@
         return [hi, (x - hi.astype(f32)).astype(bf16)]
 
     def project(s, c):
-        st = starts[s]
+        st = starts[pl.ds(s, 1), :]
         v = g[s] - dual[s]
         lead_v = v * st
         tail_v = v * v * (1.0 - st)
@@ -346,6 +345,8 @@
             return c
 
         lax.fori_loop(0, S, back, 0)
+        for i in range(n_scen):
+            snd[i] = acc[i].astype(bf16)
         for j in SJ:
             d_rs1(j).start()
 
@@ -356,7 +357,7 @@
         tot = acc[ms]
         for j in SJ:
             d_rs1(j).wait_recv()
-            tot = tot + rs1[j - 1]
+            tot = tot + rs1[j - 1].astype(f32)
         for j in SJ:
             d_rs1(j).wait_send()
 
@@ -364,7 +365,7 @@
         def _():
             res1[...] = tot - cost1[:, pl.ds(pl.multiple_of(ms * SH, 128), SH)]
             for s in range(S):
-                res2[s] = back2[s] - cost2[s]
+                res2[s] = back2[s] - cost2[s:s + 1, :]
 
         @pl.when(step != 0)
         def _():
@@ -455,30 +456,23 @@
                 p = lax.dot_general(x, tech[s, rows, :], dn, preferred_element_type=f32)
                 p = p + lax.dot_general(y, rec[s, rows, :], dn, preferred_element_type=f32)
                 part[s, k] = p.astype(bf16)
-            for j in CJ:
-                d_rsc(j, s).start()
 
             @pl.when(s == 0)
             def _():
                 norm_forward()
 
-            @pl.when(s == LAG - 1)
-            def _():
-                norm_finish()
-
-            @pl.when(s >= LAG)
-            def _():
-                process(s - LAG)
-
+            for j in CJ:
+                d_rsc(j, s).start()
             return c
 
         lax.fori_loop(0, S, front, 0)
+        norm_finish()
 
         def drain(s, c):
             process(s)
             return c
 
-        lax.fori_loop(S - LAG, S, drain, 0)
+        lax.fori_loop(0, S, drain, 0)
         crv_own[...] = pack(qq[...])
         for j in CJ:
             d_c1(j).start()
@@ -542,7 +536,7 @@
         V((S, NCONE, R), bf16),
         V((S, n_col, B, RQ), bf16), V((S, n_col, B, RQ), bf16), V((nc, S, B, RQ), bf16),
         V((S, B, RQ), f32),
-        V((n_scen, B, SH), f32), V((ns, B, SH), f32), V((n_scen, B, SH), bf16),
+        V((n_scen, B, SH), f32), V((n_scen, B, SH), bf16), V((ns, B, SH), bf16), V((n_scen, B, SH), bf16),
         V((S, B, C2), f32), V((S, B, C2), f32), V((S, B, C2), f32),
         V((B, SH), f32), V((B, SH), f32),
         V((8, 128), f32), V((ns, 8, 128), f32), V((8, 128), f32), V((nc, 8, 128), f32),
@@ -569,8 +563,7 @@
             collective_id=0, has_side_effects=True, vmem_limit_bytes=58 * 1024 * 1024),
     )(
         tech, recourse, jnp.transpose(rhs, (1, 0, 2)),
-        cost_first.reshape(1, C1), cost_second.reshape(S, 1, C2),
-        cone_id.reshape(S, 1, R), starts.reshape(S, 1, R),
+        cost_first.reshape(1, C1), cost_second, cone_id, starts,
     )
     back = lambda a: jnp.transpose(a, (1, 0, 2))
     return x, back(y), back(slack), back(dual)

time: 383 us -> 366 us (0.956)
  Pallas kernels: 368 us -> 354 us
    pallas_call x1, Pallas kernels: 368 us -> 354 us  [fused(): pl.pallas_call(functools.partial(kernel_body, (n_scen, n_col, B, S, R, C1...]
where the time goes in v2:
time: 366 us
  Pallas kernels  354 us (97%)
  local copies, waits for them, and re-layouts  9.68 us (3%)
    pallas_call x1, Pallas kernels, fused(): pl.pallas_call(functools.partial(kernel_body, (n_scen, n_col, B, S, R, C1...  354 us
    unnamed x5, local copies, waits for them, and re-layouts  9.68 us

profile of v2, /device:TPU:0, one launch (start us, length us, event | category | flops | bytes accessed | tf_op | source)
XLA Modules:
  0.0 365.5 jit_solution(17703194291456219605)
XLA Ops:
  0.6 0.9 slice_compare_fusion
  1.6 0.7 pad_convert_fusion.starts
  2.3 2.8 copy.15
  5.1 353.6 %shard_map.93 = (f32[32,1024]{1,0:T(8,128)}, f32[4,32,256]{2,1,0:T(8,128)}, f32[4,32,512]{2,1,0:T(8,128)}, f32[4,32,512]{2,1,0:T(8,128)}) custom-call(bf16[4,2048,1024]{2,1,0:T(8,128)(2,1)} %tech_hbm.1, bf16[4,2048,256]{2,1,0:T(8,128)(2,1)} %rec_hbm.1, f32[4,32,2048]{2,1,0:T(8,128)} %bitcast.7, f32[1,1024]{1,0:T(1,128)} %bitcast.11, f32[4,256]{1,0:T(4,128)} %cost2.1, ...), custom_call_target="tpu_custom_call" | custom-call | tf_op jit(solution)/shard_map/pallas_call | solution.py:551
  358.7 1.6 copy.11
  360.3 1.8 copy.12
  362.1 1.8 copy.13
  364.0 1.6 copy.17
